TPU v7x, 256 devices: a whole 4x4x8 slice. The times are simulated.
256 devices in a mesh: dp: 64 (over z, y, core), tensor: 4 (over x).
Axes of the slice: x: 4, y: 4, z: 8, core: 2. Of those that a mesh axis runs over, the one named last changes fastest.
Arguments:
- tokens: bfloat16 [131072, 4096], P('dp', 'tensor'), may hold values from -16 to 16
- cotangent: bfloat16 [131072, 1536], P('dp', 'tensor'), may hold values from -0.059814453 to 0.059814453
- seg_start: int32 [64, 2], P('dp'), may hold values from 0 to 1024, as said below
- seg_length: int32 [64, 2], P('dp'), may hold values from 0 to 1024, as said below
Outputs:
- weight_grad: float32 [4096, 2, 1536], P('dp', None, 'tensor')
Inputs may be any that keep to these rules, and one draw needn't show every extreme that they name: Within each index of dp the 2 segments lie in expert order, packed from row 0 without gaps: seg_start is the running sum of seg_length before each expert. `seg_length`: each length is at most 1024; in every draw some expert on some index of dp has exactly 1024 rows. Rows after the last segment belong to no expert.
All inputs are finite; a program needn't handle non-finite values.
Results may differ from a plain program's by a relative error of at most 0.0003.
Values may be sent and summed in bfloat16 or wider, within the bound.
A program may use at most 128 MiB of HBM per device.

v0:
```python
import jax
import jax.numpy as jnp
from jax import lax
from jax.sharding import PartitionSpec as P

E_W = 2
CAP = 1024


def block_term(columns, grads, lower, upper, size):
    total_rows = columns.shape[0]
    first = jnp.minimum(lower, total_rows - size)
    rows = first + jnp.arange(size, dtype=jnp.int32)
    keep = (rows >= lower) & (rows < upper)
    block_x = lax.dynamic_slice_in_dim(columns, first, size, 0)
    block_g = lax.dynamic_slice_in_dim(grads, first, size, 0)
    block_g = jnp.where(keep[:, None], block_g, jnp.zeros_like(block_g))
    return lax.dot_general(
        block_x, block_g, (((0,), (0,)), ((), ())), preferred_element_type=jnp.float32
    )


def expert_term(columns, grads, start, length):
    return block_term(columns, grads, start, start + length, CAP)


def all_experts(columns, grads, seg_start, seg_length):
    terms = [
        expert_term(columns, grads, seg_start[0, expert], seg_length[0, expert])
        for expert in range(E_W)
    ]
    return jnp.stack(terms, 1)


def per_device(tokens, cotangent, seg_start, seg_length):
    whole = lax.all_gather(tokens, "tensor", axis=1, tiled=True)
    terms = all_experts(whole, cotangent, seg_start, seg_length)
    return lax.psum_scatter(terms, "dp", scatter_dimension=0, tiled=True)


def solution(mesh):
    in_specs = (P("dp", "tensor"), P("dp", "tensor"), P("dp", None), P("dp", None))
    out_specs = P("dp", None, "tensor")
    return jax.shard_map(
        per_device, mesh=mesh, in_specs=in_specs, out_specs=out_specs, check_vma=False
    )
```

profile of v0, /device:TPU:5, one launch (start us, length us, event | category | flops | bytes accessed | tf_op | source)
XLA Modules:
  0.0 358.7 jit_solution(13309784438821969683)
XLA Ops:
  6.5 0.0 all-gather.2.cloned.1.call-start
  6.5 0.7 all-gather.2.cloned.1.call-update
  7.3 0.0 reduce-scatter.2.cloned.1.call-start
  7.3 1.4 fusion.29
  10.0 1.3 fusion.28
  13.9 0.7 fusion.22
  14.5 0.7 fusion.23
  15.2 153.0 %all-gather.2.cloned.1.call-done = bf16[2048,4096]{1,0:T(8,128)(2,1)} async-done(((bf16[2048,1024]{1,0:T(8,128)(2,1)}), bf16[2048,4096]{1,0:T(8,128)(2,1)}) %all-gather.2.cloned.1.call-update) | async-done | bytes 16777232 | tf_op jit(solution)/shard_map/all_gather | solution.py:36
  168.2 0.0 copy-start
  168.2 0.0 copy-start.1
  168.2 7.5 %fusion.7 = f32[4096,1,384]{2,0,1:T(8,128)S(1)} fusion(bf16[2048,4096]{1,0:T(8,128)(2,1)} %all-gather.2.cloned.1.call-done, s32[]{:T(128)S(6)} %select_n.17, bf16[2048,384]{1,0:T(8,128)(2,1)} %param.5, pred[1024]{0:T(1024)(128)(4,1)S(1)} %fusion.23), kind=kOutput, calls=%fused_computation.6 | convolution fusion | flops 3221618688 | bytes 15468544 | tf_op jit(solution)/shard_map/dot_general | solution.py:18
  175.8 0.9 copy-done
  176.7 0.4 copy-done.1
  177.1 6.7 %fusion.4 = f32[4096,1,384]{2,0,1:T(8,128)} fusion(bf16[2048,4096]{1,0:T(8,128)(2,1)S(1)} %copy-done, s32[]{:T(128)S(6)} %select_n.15, bf16[2048,384]{1,0:T(8,128)(2,1)S(1)} %copy-done.1, pred[1024]{0:T(1024)(128)(4,1)S(1)} %fusion.22), kind=kOutput, calls=%fused_computation.5 | convolution fusion | flops 3221618688 | bytes 15468544 | tf_op jit(solution)/shard_map/dot_general | solution.py:18
  183.8 8.1 %pad_maximum_fusion = f32[4096,2,384]{2,0,1:T(8,128)} fusion(f32[4096,1,384]{2,0,1:T(8,128)S(1)} %fusion.7, f32[4096,1,384]{2,0,1:T(8,128)} %fusion.4), kind=kLoop, calls=%fused_computation | loop fusion | flops 3145728 | bytes 25165824 | tf_op jit(solution)/shard_map/stack | solution.py:32
  191.9 0.0 reduce-scatter.2.cloned.1.call-update
  191.9 158.1 %reduce-scatter.2.cloned.1.call-done = f32[64,2,384]{2,0,1:T(8,128)} async-done(((f32[4096,2,384]{2,0,1:T(8,128)}), f32[64,2,384]{2,0,1:T(8,128)}) %reduce-scatter.2.cloned.1.call-update) | async-done | bytes 196624 | tf_op jit(solution)/shard_map/reduce_scatter | solution.py:38
  350.1 1.8 copy.5
Async XLA Ops:
  6.5 161.7 %all-gather.2.cloned.1.call-start = ((), (), s32[]{:S(2)}) async-start(), calls=%async_computation.1 | async-start | bytes 20971520 | tf_op jit(solution)/shard_map/all_gather | solution.py:36
  7.3 342.8 %reduce-scatter.2.cloned.1.call-start = ((), (), s32[]{:S(2)}) async-start(), calls=%async_computation.2 | async-start | bytes 12779520 | tf_op jit(solution)/shard_map/reduce_scatter | solution.py:38
  168.2 8.5 %copy-start = (bf16[2048,4096]{1,0:T(8,128)(2,1)S(1)}, bf16[2048,4096]{1,0:T(8,128)(2,1)}, u32[]{:S(2)}) copy-start(bf16[2048,4096]{1,0:T(8,128)(2,1)} %all-gather.2.cloned.1.call-done) | copy-start | bytes 50331652
  168.2 8.9 %copy-start.1 = (bf16[2048,384]{1,0:T(8,128)(2,1)S(1)}, bf16[2048,384]{1,0:T(8,128)(2,1)}, u32[]{:S(2)}) copy-start(bf16[2048,384]{1,0:T(8,128)(2,1)} %param.5) | copy-start | bytes 4718596
Sparse Core Ops, SparseCore 0:
  9.1 159.0 all-gather.1
  192.0 157.9 reduce-scatter.1
where the time goes:
time: 364 us; the launch traced here: 359 us
  waiting for transfers between devices  312 us (86%)
  between operations  17.3 us (5%)
  matrix products  14.2 us (4%)
  other arithmetic  9.47 us (3%)
  local copies, waits for them, and re-layouts  5.8 us (2%)
    reduce_scatter x1, waiting for transfers between devices, per_device(): return lax.psum_scatter(terms, 'dp', scatter_dimension=0, tiled=True)  158 us
    all_gather x1, waiting for transfers between devices, per_device(): whole = lax.all_gather(tokens, 'tensor', axis=1, tiled=True)  153 us
    dot_general x2, matrix products, block_term(): lax.dot_general(block_x, block_g, (((0,), (0,)), ((), ())), preferred_ele...  14.2 us
    another operation x1, other arithmetic, all_experts(): return jnp.stack(terms, 1)  8.12 us
  transfers between devices with their start and end apart: 2, of which 2 were waited for; matrix products, arithmetic and copies ran while one was open for 1% of the time, Pallas kernels for 0%

commit v1 on v0

v1 whole, which is shorter than its diff:
```python
import jax
import jax.numpy as jnp
from jax import lax
from jax.experimental import pallas as pl
from jax.experimental.pallas import tpu as pltpu
from jax.sharding import PartitionSpec as P

MESH = pl.DeviceIdType.MESH
CAP = 1024
FEATS = 1024
L = 128
SUBS = 3
OWN, LEFT, RIGHT, OPP = 0, 1, 2, 3
X_OFF = {OWN: 0, LEFT: 3, RIGHT: 1, OPP: 2}
ORDER = (
    [(OWN, s) for s in range(SUBS)]
    + [(side, s) for s in range(SUBS) for side in (LEFT, RIGHT)]
    + [(OPP, s) for s in range(SUBS)]
)
N_Q = len(ORDER)
Q_OF = {slot_s: q for q, slot_s in enumerate(ORDER)}
BLOCKS = FEATS // L


def kernel(
    tok_hbm, cot_hbm, start_ref, length_ref, out_ref,
    xin, gin, xt, xsend, gbuf, gsend, p, y1, y2, zb, fin, ob,
    in_sem, gd_s, gd_r, xd_s, xd_r, gx_s, gx_r, y1_s, y1_r, y2_s, y2_r, z_s, z_r, f_s, f_r,
):
    t = lax.axis_index("tensor")
    dp = lax.axis_index("dp")
    z, y, e = dp // 8, (dp // 2) % 4, dp % 2

    def dev(x, y, z, c):
        return (z * 8 + y * 2 + c, x)

    def remote(src, dst, s, r, to):
        return pltpu.make_async_remote_copy(
            src_ref=src, dst_ref=dst, send_sem=s, recv_sem=r, device_id=to, device_id_type=MESH
        )

    def wait(ref, sem):
        pltpu.make_async_copy(ref, ref, sem).wait()

    partner = dev(t, y, z, 1 - e)
    right, left = dev((t + 1) % 4, y, z, e), dev((t + 3) % 4, y, z, e)
    y_a, y_b = y + 1 - 2 * (y % 2), 3 - y
    dev_a, dev_b = dev(t, y_a, z, e), dev(t, y_b, z, e)
    dest_z, dest_c = 2 * t + z // 4, (z // 2) % 2
    own_dest = (dest_z == z) & (dest_c == e)

    g_load = pltpu.make_async_copy(cot_hbm, gin, in_sem.at[0])
    x_load = pltpu.make_async_copy(tok_hbm, xin, in_sem.at[1])
    g_load.start()
    x_load.start()

    barrier = pltpu.get_barrier_semaphore()

    def greet(to):
        pl.semaphore_signal(barrier, inc=1, device_id=to, device_id_type=MESH)

    for to in (partner, right, left, dev_a, dev_b):
        greet(to)
    for d in range(1, 8):
        greet(dev(t, y, (z + d) % 8, e))
    for half in range(2):
        for c in range(2):
            sx, sz = z // 2, 4 * (z % 2) + 2 * e + half

            @pl.when(jnp.logical_not((sx == t) & (sz == z) & (c == e)))
            def _():
                greet(dev(sx, y, sz, c))

    def bounds(expert):
        first = start_ref[0, expert]
        return first, first + length_ref[0, expert]

    def pick(low, high, row, first):
        return jnp.where(row >= first, low, high)

    row = lax.broadcasted_iota(jnp.int32, (CAP, L), 0)
    (f0, l0), (f1, l1) = bounds(0), bounds(1)
    first_me, last_me = f0 + e * (f1 - f0), l0 + e * (l1 - l0)
    first_it, last_it = f1 + e * (f0 - f1), l1 + e * (l0 - l1)

    def cot_of(s, first, last):
        low = gin[:CAP, s * L : (s + 1) * L].astype(jnp.float32)
        high = gin[CAP:, s * L : (s + 1) * L].astype(jnp.float32)
        source_row = row + jnp.where(row >= first, 0, CAP)
        value = jnp.where(source_row < last, pick(low, high, row, first), 0.0)
        return value.astype(jnp.bfloat16)

    g_load.wait()
    for s in range(SUBS):
        gsend[s] = cot_of(s, first_it, last_it)
        gbuf[s, e] = cot_of(s, first_me, last_me)
    pl.semaphore_wait(barrier, 16 - jnp.where(own_dest, 1, 0))

    def give(s, src):
        unit = gbuf.at[s, src]
        q = Q_OF[LEFT, s]
        remote(unit, gbuf.at[q, src], gx_s.at[s, 0, src], gx_r.at[q - SUBS, src], right).start()
        q = Q_OF[RIGHT, s]
        remote(unit, gbuf.at[q, src], gx_s.at[s, 1, src], gx_r.at[q - SUBS, src], left).start()

    for s in range(SUBS):
        remote(gsend.at[s], gbuf.at[s, e], gd_s.at[s], gd_r.at[s], partner).start()
    give(0, e)
    for s in range(SUBS):
        wait(gbuf.at[s, 1 - e], gd_r.at[s])
        give(s, 1 - e)
        if s + 1 < SUBS:
            give(s + 1, e)

    x_load.wait()
    for fb in range(BLOCKS):
        cols = slice(fb * L, (fb + 1) * L)
        low = xin[:CAP, cols].astype(jnp.float32)
        high = xin[CAP:, cols].astype(jnp.float32)
        xsend[cols, :] = pick(low, high, row, first_it).T.astype(jnp.bfloat16)
        remote(xsend.at[cols, :], xt.at[e, cols, :], xd_s, xd_r, partner).start()
        xt[e, cols, :] = pick(low, high, row, first_me).T.astype(jnp.bfloat16)
    wait(xt.at[1 - e], xd_r)

    def multiply(q):
        slot, s = ORDER[q]
        if slot != OWN:
            for src in range(2):
                wait(gbuf.at[q, src], gx_r.at[q - SUBS, src])
        o = Q_OF[OPP, s]
        if slot == LEFT:
            remote(gbuf.at[q, 0], gbuf.at[o, 0], gx_s.at[s, 2, 0], gx_r.at[o - SUBS, 0], right).start()
        if slot == RIGHT:
            remote(gbuf.at[q, 1], gbuf.at[o, 1], gx_s.at[s, 2, 1], gx_r.at[o - SUBS, 1], left).start()

        def block(m, carry):
            rows = pl.ds(pl.multiple_of(m * L, L), L)
            p[q, m] = jnp.dot(
                xt[0, rows, :], gbuf[q, 0], preferred_element_type=jnp.float32
            ) + jnp.dot(xt[1, rows, :], gbuf[q, 1], preferred_element_type=jnp.float32)
            return carry

        lax.fori_loop(0, BLOCKS, block, 0)
        remote(p.at[q, 3 - y_a], y1.at[q, 0, 1], y1_s.at[q], y1_r.at[q], dev_a).start()
        remote(p.at[q, 4 + y_b + 1 - 2 * (y_b % 2)], y1.at[q, 1, 1], y1_s.at[q], y1_r.at[q], dev_b).start()
        remote(p.at[q, y_a], y1.at[q, 0, 0], y1_s.at[q], y1_r.at[q], dev_a).start()
        remote(p.at[q, 4 + y_b], y1.at[q, 1, 0], y1_s.at[q], y1_r.at[q], dev_b).start()

    def second(q):
        wait(y1.at[q], y1_r.at[q])
        p[q, y_b] += y1[q, 0, 1]
        remote(p.at[q, y_b], y2.at[q, 0], y2_s.at[q], y2_r.at[q], dev_b).start()
        p[q, 4 + y_a] += y1[q, 1, 1]
        remote(p.at[q, 4 + y_a], y2.at[q, 1], y2_s.at[q], y2_r.at[q], dev_a).start()
        p[q, y] += y1[q, 0, 0]
        p[q, 4 + y] += y1[q, 1, 0]

    def piece(q, zz):
        return p.at[q, (zz // 4) * 4 + y, pl.ds(pl.multiple_of((zz % 4) * 32, 32), 32), :]

    def third(q):
        wait(y2.at[q], y2_r.at[q])
        p[q, y] += y2[q, 0]
        p[q, 4 + y] += y2[q, 1]
        for d in (4, 3, 5, 2, 6, 1, 7):
            zz = (z + d) % 8
            remote(piece(q, zz), zb.at[q, d - 1], z_s.at[q], z_r.at[q], dev(t, y, zz, e)).start()

    def last(q):
        slot, s = ORDER[q]
        wait(zb.at[q], z_r.at[q])
        total = piece(q, z)[...]
        for d in range(7):
            total += zb[q, d]
        fin[q] = total
        to = dev((t + X_OFF[slot]) % 4, y, dest_z, dest_c)
        place = ob.at[e, s, z % 2]
        if slot == OWN:

            @pl.when(own_dest)
            def _():
                pltpu.make_async_copy(fin.at[q], place, f_r).start()

            @pl.when(jnp.logical_not(own_dest))
            def _():
                remote(fin.at[q], place, f_s.at[q], f_r, to).start()
        else:
            remote(fin.at[q], place, f_s.at[q], f_r, to).start()

    for step in range(N_Q + 3):
        if step < N_Q:
            multiply(step)
        if 0 <= step - 1 < N_Q:
            second(step - 1)
        if 0 <= step - 2 < N_Q:
            third(step - 2)
        if 0 <= step - 3 < N_Q:
            last(step - 3)

    wait(ob, f_r)
    for c in range(2):
        for s in range(SUBS):
            for half in range(2):
                out_ref[c, half * 32 : (half + 1) * 32, s * L : (s + 1) * L] = ob[c, s, half]

    for s in range(SUBS):
        wait(gsend.at[s], gd_s.at[s])
        for way in range(3):
            for src in range(2):
                wait(gbuf.at[s, src], gx_s.at[s, way, src])
    wait(xsend, xd_s)
    for q in range(N_Q):
        wait(y1.at[q], y1_s.at[q])
        wait(y2.at[q], y2_s.at[q])
        wait(zb.at[q], z_s.at[q])
        if ORDER[q][0] == OWN:

            @pl.when(jnp.logical_not(own_dest))
            def _():
                wait(fin.at[q], f_s.at[q])
        else:
            wait(fin.at[q], f_s.at[q])


def per_device(tokens, cotangent, seg_start, seg_length):
    dma = pltpu.SemaphoreType.DMA
    bf16, f32 = jnp.bfloat16, jnp.float32
    out = pl.pallas_call(
        kernel,
        out_shape=jax.ShapeDtypeStruct((2, 64, SUBS * L), f32),
        in_specs=[pl.BlockSpec(memory_space=pl.ANY)] * 2 + [pl.BlockSpec(memory_space=pltpu.SMEM)] * 2,
        out_specs=pl.BlockSpec(memory_space=pltpu.VMEM),
        scratch_shapes=[
            pltpu.VMEM((2 * CAP, FEATS), bf16),
            pltpu.VMEM((2 * CAP, SUBS * L), bf16),
            pltpu.VMEM((2, FEATS, CAP), bf16),
            pltpu.VMEM((FEATS, CAP), bf16),
            pltpu.VMEM((N_Q, 2, CAP, L), bf16),
            pltpu.VMEM((SUBS, CAP, L), bf16),
            pltpu.VMEM((N_Q, BLOCKS, L, L), f32),
            pltpu.VMEM((N_Q, 2, 2, L, L), f32),
            pltpu.VMEM((N_Q, 2, L, L), f32),
            pltpu.VMEM((N_Q, 7, 32, L), f32),
            pltpu.VMEM((N_Q, 32, L), f32),
            pltpu.VMEM((2, SUBS, 2, 32, L), f32),
            dma((2,)),
            dma((SUBS,)), dma((SUBS,)), dma, dma,
            dma((SUBS, 3, 2)), dma((N_Q - SUBS, 2)),
            dma((N_Q,)), dma((N_Q,)), dma((N_Q,)), dma((N_Q,)), dma((N_Q,)), dma((N_Q,)),
            dma((N_Q,)), dma,
        ],
        compiler_params=pltpu.CompilerParams(
            collective_id=0, has_side_effects=True, vmem_limit_bytes=60 * 1024 * 1024
        ),
        cost_estimate=pl.CostEstimate(flops=6442450944, bytes_accessed=6000000, transcendentals=0),
    )(tokens, cotangent, seg_start, seg_length)
    return out.transpose(1, 0, 2)


def solution(mesh):
    in_specs = (P("dp", "tensor"), P("dp", "tensor"), P("dp", None), P("dp", None))
    out_specs = P("dp", None, "tensor")
    return jax.shard_map(
        per_device, mesh=mesh, in_specs=in_specs, out_specs=out_specs, check_vma=False
    )
```

time: 364 us -> 91.6 us (0.25); the launches traced: 359 us -> 91.2 us
  waiting for transfers between devices: 312 us -> 0 us
  Pallas kernels: 0 us -> 89.4 us
  between operations: 17.3 us -> 0.01 us
  matrix products: 14.2 us -> 0 us
  other arithmetic: 9.47 us -> 0 us
  local copies, waits for them, and re-layouts: 5.8 us -> 1.76 us
    reduce_scatter x1 -> x0, waiting for transfers between devices: 158 us -> none  [per_device(): return lax.psum_scatter(terms, 'dp', scatter_dimension=0, tiled=True)]
    all_gather x1 -> x0, waiting for transfers between devices: 153 us -> none  [per_device(): whole = lax.all_gather(tokens, 'tensor', axis=1, tiled=True)]
    pallas_call x0 -> x1, Pallas kernels: none -> 89.4 us  [per_device(): pl.pallas_call(kernel, out_shape=jax.ShapeDtypeStruct((2, 64, SUBS * L),...]
    dot_general x2 -> x0, matrix products: 14.2 us -> none  [block_term(): lax.dot_general(block_x, block_g, (((0,), (0,)), ((), ())), preferred_ele...]
    another operation x1 -> x0, other arithmetic: 8.12 us -> none  [all_experts(): return jnp.stack(terms, 1)]
  transfers between devices with their start and end apart: 2 -> 0, of which waited for: 2 -> 0; matrix products, arithmetic and copies ran while one was open for 1% -> 0% of each run, Pallas kernels for 0% -> 0%
where the time goes in v1:
time: 91.6 us; the launch traced here: 91.2 us
  Pallas kernels  89.4 us (98%)
  local copies, waits for them, and re-layouts  1.76 us (2%)
    pallas_call x1, Pallas kernels, per_device(): pl.pallas_call(kernel, out_shape=jax.ShapeDtypeStruct((2, 64, SUBS * L),...  89.4 us

profile of v1, /device:TPU:5, one launch (start us, length us, event | category | flops | bytes accessed | tf_op | source)
XLA Modules:
  0.0 91.2 jit_solution(13950087173665518841)
XLA Ops:
  0.0 89.4 %shard_map.46 = f32[2,64,384]{2,1,0:T(8,128)} custom-call(bf16[2048,1024]{1,0:T(8,128)(2,1)} %tok_hbm.1, bf16[2048,384]{1,0:T(8,128)(2,1)} %cot_hbm.1, s32[1,2]{1,0:T(1,128)} %start_ref.1, s32[1,2]{1,0:T(1,128)} %length_ref.1), custom_call_target="tpu_custom_call" | custom-call | flops 6442450944 | bytes 6000000 | tf_op jit(solution)/shard_map/pallas_call | solution.py:228
  89.4 1.8 %copy.5 = f32[64,2,384]{2,1,0:T(2,128)} copy(f32[64,2,384]{2,0,1:T(8,128)} %bitcast.1) | data formatting | bytes 393216 | tf_op jit(solution)/shard_map/transpose | solution.py:257

commit v2 on v1

v2 whole, which is shorter than its diff:
```python
import jax
import jax.numpy as jnp
from jax import lax
from jax.experimental import pallas as pl
from jax.experimental.pallas import tpu as pltpu
from jax.sharding import PartitionSpec as P

MESH = pl.DeviceIdType.MESH
CAP = 1024
FEATS = 1024
L = 128
SUBS = 3
OWN, LEFT, RIGHT, OPP = 0, 1, 2, 3
X_OFF = {OWN: 0, LEFT: 3, RIGHT: 1, OPP: 2}
ORDER = (
    [(OWN, s) for s in range(SUBS)]
    + [(side, s) for s in range(SUBS) for side in (LEFT, RIGHT)]
    + [(OPP, s) for s in range(SUBS)]
)
N_Q = len(ORDER)
Q_OF = {slot_s: q for q, slot_s in enumerate(ORDER)}
BLOCKS = FEATS // L
SPLIT = (N_Q - 1,)
PLAN = (
    "m0,1", "a1", "a0", "m2", "a2", "b1", "m3,4", "a4", "a3", "b0", "b2", "c1", "b4", "m5,6", "a5", "a6",
    "b3", "c0", "d1", "c2", "c4", "b5", "d0", "b6", "m7,8", "a8", "a7", "c3", "d2", "c5", "c6", "d4", "m9",
    "a9", "b8", "d3", "b7", "m10", "a10", "b9", "d5", "c8", "d6", "c7", "m11", "c9", "b10", "d8", "b11",
    "B11", "c10", "d7", "c11", "C11", "d9", "d10", "d11",
)
HALF = FEATS // 2


def kernel(
    tok_hbm, cot_hbm, start_ref, length_ref, out_ref,
    xin, gin, xt, xsend, gbuf, gsend, p, y1, y2, zb, fin, ob,
    in_sem, gd_s, gd_r, xd_s, xd_r, gx_s, gx_r, y1_s, y1_r, y2_s, y2_r, z_s, z_r, f_s, f_r,
):
    t = lax.axis_index("tensor")
    dp = lax.axis_index("dp")
    z, y, e = dp // 8, (dp // 2) % 4, dp % 2

    def dev(x, y, z, c):
        return (z * 8 + y * 2 + c, x)

    def remote(src, dst, s, r, to):
        return pltpu.make_async_remote_copy(
            src_ref=src, dst_ref=dst, send_sem=s, recv_sem=r, device_id=to, device_id_type=MESH
        )

    def wait(ref, sem):
        pltpu.make_async_copy(ref, ref, sem).wait()

    partner = dev(t, y, z, 1 - e)
    right, left = dev((t + 1) % 4, y, z, e), dev((t + 3) % 4, y, z, e)
    y_a, y_b = y + 1 - 2 * (y % 2), 3 - y
    dev_a, dev_b = dev(t, y_a, z, e), dev(t, y_b, z, e)

    def rank(zz):
        return (zz - 2 * t + 11) % 8

    my_rank = rank(z)
    dest_z, dest_c = 2 * t + my_rank // 4, (my_rank // 2) % 2
    own_dest = (dest_z == z) & (dest_c == e)

    g_loads = [
        pltpu.make_async_copy(cot_hbm.at[:, cols], gin.at[:, cols], in_sem.at[s])
        for s, cols in enumerate(pl.ds(s * L, L) for s in range(SUBS))
    ]
    x_loads = [
        pltpu.make_async_copy(tok_hbm.at[:, cols], xin.at[:, cols], in_sem.at[SUBS + i])
        for i, cols in enumerate(pl.ds(i * 2 * L, 2 * L) for i in range(BLOCKS // 2))
    ]
    for load in g_loads:
        load.start()

    barrier = pltpu.get_barrier_semaphore()

    def greet(to):
        pl.semaphore_signal(barrier, inc=1, device_id=to, device_id_type=MESH)

    for to in (partner, right, left, dev_a, dev_b):
        greet(to)
    for d in range(1, 8):
        greet(dev(t, y, (z + d) % 8, e))
    for half in range(2):
        for c in range(2):
            sx = z // 2
            sz = (4 * (z % 2) + 2 * e + half + 2 * sx + 5) % 8

            @pl.when(jnp.logical_not((sx == t) & (sz == z) & (c == e)))
            def _():
                greet(dev(sx, y, sz, c))

    def bounds(expert):
        first = start_ref[0, expert]
        return first, first + length_ref[0, expert]

    def pick(low, high, row, first):
        return jnp.where(row >= first, low, high)

    row = lax.broadcasted_iota(jnp.int32, (CAP, L), 0)
    (f0, l0), (f1, l1) = bounds(0), bounds(1)
    first_me, last_me = f0 + e * (f1 - f0), l0 + e * (l1 - l0)
    first_it, last_it = f1 + e * (f0 - f1), l1 + e * (l0 - l1)

    def cot_of(s, first, last):
        low = gin[:CAP, s * L : (s + 1) * L].astype(jnp.float32)
        high = gin[CAP:, s * L : (s + 1) * L].astype(jnp.float32)
        source_row = row + jnp.where(row >= first, 0, CAP)
        value = jnp.where(source_row < last, pick(low, high, row, first), 0.0)
        return value.astype(jnp.bfloat16)

    def give(s, src):
        unit = gbuf.at[s, src]
        q = Q_OF[LEFT, s]
        remote(unit, gbuf.at[q, src], gx_s.at[s, 0, src], gx_r.at[q - SUBS, src], right).start()
        q = Q_OF[RIGHT, s]
        remote(unit, gbuf.at[q, src], gx_s.at[s, 1, src], gx_r.at[q - SUBS, src], left).start()

    def to_partner(s):
        gsend[s] = cot_of(s, first_it, last_it)
        remote(gsend.at[s], gbuf.at[s, e], gd_s.at[s], gd_r.at[s], partner).start()

    g_loads[0].wait()
    for load in x_loads:
        load.start()
    gbuf[0, e] = cot_of(0, first_me, last_me)
    pl.semaphore_wait(barrier, 16 - jnp.where(own_dest, 1, 0))
    give(0, e)
    to_partner(0)
    for s in range(1, SUBS):
        g_loads[s].wait()
        to_partner(s)
        gbuf[s, e] = cot_of(s, first_me, last_me)
    for s in range(SUBS):
        wait(gbuf.at[s, 1 - e], gd_r.at[s])
        give(s, 1 - e)
        if s + 1 < SUBS:
            give(s + 1, e)

    def tokens_of(fb, first):
        cols = slice(fb * L, (fb + 1) * L)
        low = xin[:CAP, cols].astype(jnp.float32)
        high = xin[CAP:, cols].astype(jnp.float32)
        return pick(low, high, row, first).astype(jnp.bfloat16).T

    my_rows = pl.ds(pl.multiple_of(e * CAP, CAP), CAP)
    its_rows = pl.ds(pl.multiple_of((1 - e) * CAP, CAP), CAP)
    for fb in range(BLOCKS):
        if fb % 2 == 0:
            x_loads[fb // 2].wait()
        xsend[:, fb] = tokens_of(fb, first_it).reshape(2, L // 2, CAP)
        remote(xsend.at[:, fb], xt.at[:, fb, :, my_rows], xd_s, xd_r, partner).start()
    for fb in range(BLOCKS):
        xt[:, fb, :, my_rows] = tokens_of(fb, first_me).reshape(2, L // 2, CAP)
    wait(xt.at[:, :, :, its_rows], xd_r)

    def receive(q):
        slot, s = ORDER[q]
        if slot != OWN:
            for src in range(2):
                wait(gbuf.at[q, src], gx_r.at[q - SUBS, src])
        o = Q_OF[OPP, s]
        if slot == LEFT:
            remote(gbuf.at[q, 0], gbuf.at[o, 0], gx_s.at[s, 2, 0], gx_r.at[o - SUBS, 0], right).start()
        if slot == RIGHT:
            remote(gbuf.at[q, 1], gbuf.at[o, 1], gx_s.at[s, 2, 1], gx_r.at[o - SUBS, 1], left).start()

    def multiply(group, part):
        grads = jnp.concatenate([gbuf[q].reshape(2 * CAP, L) for q in group], axis=1)
        terms = jnp.dot(
            xt[part].reshape(HALF, 2 * CAP), grads, preferred_element_type=jnp.float32
        )
        for k, q in enumerate(group):
            p[q, :, part] = terms[:, k * L : (k + 1) * L].reshape(BLOCKS, 2, 32, L)

    def view(ref, q, part, *at):
        return ref.at[q, *at, part] if q in SPLIT else ref.at[q, *at]

    def first(q, part=0):
        for m, h, b, to in (
            (3 - y_a, 0, 1, dev_a),
            (4 + y_b + 1 - 2 * (y_b % 2), 1, 1, dev_b),
            (y_a, 0, 0, dev_a),
            (4 + y_b, 1, 0, dev_b),
        ):
            remote(view(p, q, part, m), view(y1, q, part, h, b), y1_s.at[q + part], y1_r.at[q + part], to).start()

    def second(q, part=0):
        wait(view(y1, q, part, slice(None), slice(None)), y1_r.at[q + part])
        for m, h, to in ((y_b, 0, dev_b), (4 + y_a, 1, dev_a)):
            view(p, q, part, m)[...] += view(y1, q, part, h, 1)[...]
            remote(view(p, q, part, m), view(y2, q, part, h), y2_s.at[q + part], y2_r.at[q + part], to).start()
        for m, h in ((y, 0), (4 + y, 1)):
            view(p, q, part, m)[...] += view(y1, q, part, h, 0)[...]

    def piece(q, r):
        return p.at[q, (r // 4) * 4 + y, (r // 2) % 2, r % 2]

    def third(q, part=0):
        wait(view(y2, q, part, slice(None)), y2_r.at[q + part])
        for m, h in ((y, 0), (4 + y, 1)):
            view(p, q, part, m)[...] += view(y2, q, part, h)[...]
        if q not in SPLIT:
            for d in (4, 3, 5, 2, 6, 1, 7):
                zz = (z + d) % 8
                remote(piece(q, rank(zz)), zb.at[q, d - 1], z_s.at[q], z_r.at[q], dev(t, y, zz, e)).start()
            return
        for r in (2 * part, 2 * part + 1, 2 * part + 4, 2 * part + 5):
            zz = (r + 2 * t + 5) % 8

            @pl.when(zz != z)
            def _():
                slot = (zz - z + 7) % 8
                remote(piece(q, r), zb.at[q, slot], z_s.at[q], z_r.at[q], dev(t, y, zz, e)).start()

    def last(q):
        slot, s = ORDER[q]
        wait(zb.at[q], z_r.at[q])
        total = piece(q, my_rank)[...]
        for d in range(7):
            total += zb[q, d]
        fin[q] = total
        to = dev((t + X_OFF[slot]) % 4, y, dest_z, dest_c)
        place = ob.at[e, s, my_rank % 2]
        if slot == OWN:

            @pl.when(own_dest)
            def _():
                pltpu.make_async_copy(fin.at[q], place, f_r).start()

            @pl.when(jnp.logical_not(own_dest))
            def _():
                remote(fin.at[q], place, f_s.at[q], f_r, to).start()
        else:
            remote(fin.at[q], place, f_s.at[q], f_r, to).start()

    stages = {"a": first, "b": second, "c": third, "d": last}
    for entry in PLAN:
        qs = [int(v) for v in entry[1:].split(",")]
        if entry[0] == "m":
            for q in qs:
                receive(q)
            for part in range(2):
                multiply(qs, part)
            if qs[0] in SPLIT:
                first(qs[0], 0)
                first(qs[0], 1)
        elif entry[0].isupper():
            stages[entry[0].lower()](qs[0], 1)
        else:
            stages[entry[0]](qs[0])

    for s in range(SUBS):
        wait(gsend.at[s], gd_s.at[s])
        for way in range(3):
            for src in range(2):
                wait(gbuf.at[s, src], gx_s.at[s, way, src])
    wait(xsend, xd_s)
    for q in range(N_Q):
        for part in range(2 if q in SPLIT else 1):
            wait(view(y1, q, part, slice(None), slice(None)), y1_s.at[q + part])
            wait(view(y2, q, part, slice(None)), y2_s.at[q + part])
        wait(zb.at[q], z_s.at[q])

    wait(ob, f_r)
    for c in range(2):
        for s in range(SUBS):
            for half in range(2):
                out_ref[c, half * 32 : (half + 1) * 32, s * L : (s + 1) * L] = ob[c, s, half]
    for q in range(N_Q):
        if ORDER[q][0] == OWN:

            @pl.when(jnp.logical_not(own_dest))
            def _():
                wait(fin.at[q], f_s.at[q])
        else:
            wait(fin.at[q], f_s.at[q])


def per_device(tokens, cotangent, seg_start, seg_length):
    dma = pltpu.SemaphoreType.DMA
    bf16, f32 = jnp.bfloat16, jnp.float32
    out = pl.pallas_call(
        kernel,
        out_shape=jax.ShapeDtypeStruct((2, 64, SUBS * L), f32),
        in_specs=[pl.BlockSpec(memory_space=pl.ANY)] * 2 + [pl.BlockSpec(memory_space=pltpu.SMEM)] * 2,
        out_specs=pl.BlockSpec(memory_space=pltpu.VMEM),
        scratch_shapes=[
            pltpu.VMEM((2 * CAP, FEATS), bf16),
            pltpu.VMEM((2 * CAP, SUBS * L), bf16),
            pltpu.VMEM((2, BLOCKS, L // 2, 2 * CAP), bf16),
            pltpu.VMEM((2, BLOCKS, L // 2, CAP), bf16),
            pltpu.VMEM((N_Q, 2, CAP, L), bf16),
            pltpu.VMEM((SUBS, CAP, L), bf16),
            pltpu.VMEM((N_Q, BLOCKS, 2, 2, 32, L), f32),
            pltpu.VMEM((N_Q, 2, 2, 2, 2, 32, L), f32),
            pltpu.VMEM((N_Q, 2, 2, 2, 32, L), f32),
            pltpu.VMEM((N_Q, 7, 32, L), f32),
            pltpu.VMEM((N_Q, 32, L), f32),
            pltpu.VMEM((2, SUBS, 2, 32, L), f32),
            dma((SUBS + BLOCKS // 2,)),
            dma((SUBS,)), dma((SUBS,)), dma, dma,
            dma((SUBS, 3, 2)), dma((N_Q - SUBS, 2)),
            dma((N_Q + 1,)), dma((N_Q + 1,)), dma((N_Q + 1,)), dma((N_Q + 1,)), dma((N_Q,)), dma((N_Q,)),
            dma((N_Q,)), dma,
        ],
        compiler_params=pltpu.CompilerParams(
            collective_id=0, has_side_effects=True, vmem_limit_bytes=54000 * 1024
        ),
        cost_estimate=pl.CostEstimate(flops=6442450944, bytes_accessed=6000000, transcendentals=0),
    )(tokens, cotangent, seg_start, seg_length)
    return out.transpose(1, 0, 2)


def solution(mesh):
    in_specs = (P("dp", "tensor"), P("dp", "tensor"), P("dp", None), P("dp", None))
    out_specs = P("dp", None, "tensor")
    return jax.shard_map(
        per_device, mesh=mesh, in_specs=in_specs, out_specs=out_specs, check_vma=False
    )
```

time: 91.6 us -> 88.2 us (0.963)
  Pallas kernels: 89.4 us -> 85.7 us
    pallas_call x1, Pallas kernels: 89.4 us -> 85.7 us  [per_device(): pl.pallas_call(kernel, out_shape=jax.ShapeDtypeStruct((2, 64, SUBS * L),...]
    unnamed x0 -> x4, local copies, waits for them, and re-layouts: none -> 1.31 us
    transpose x1, local copies, waits for them, and re-layouts: 1.76 us -> 0.83 us  [per_device(): return out.transpose(1, 0, 2)]
where the time goes in v2:
time: 88.2 us; the launch traced here: 87.9 us
  Pallas kernels  85.7 us (97%)
  local copies, waits for them, and re-layouts  2.14 us (2%)
    pallas_call x1, Pallas kernels, per_device(): pl.pallas_call(kernel, out_shape=jax.ShapeDtypeStruct((2, 64, SUBS * L),...  85.7 us

profile of v2, /device:TPU:5, one launch (start us, length us, event | category | flops | bytes accessed | tf_op | source)
XLA Modules:
  0.0 87.9 jit_solution(15374916588223647535)
XLA Ops:
  0.0 0.0 copy-start
  0.0 0.7 copy-done
  0.7 0.0 copy-start.1
  0.7 0.7 copy-done.1
  1.3 85.7 %shard_map.46 = f32[2,64,384]{2,1,0:T(8,128)S(1)} custom-call(bf16[2048,1024]{1,0:T(8,128)(2,1)} %tok_hbm.1, bf16[2048,384]{1,0:T(8,128)(2,1)} %cot_hbm.1, s32[1,2]{1,0:T(1,128)S(1)} %copy-done, s32[1,2]{1,0:T(1,128)S(1)} %copy-done.1), custom_call_target="tpu_custom_call" | custom-call | flops 6442450944 | bytes 6000000 | tf_op jit(solution)/shard_map/pallas_call | solution.py:284
  87.0 0.8 copy.5
Async XLA Ops:
  0.0 0.7 copy-start
  0.7 0.7 copy-start.1

commit v3 on v2

--- a/solution.py
+++ b/solution.py
@@ -22,10 +22,10 @@
 BLOCKS = FEATS // L
 SPLIT = (N_Q - 1,)
 PLAN = (
-    "m0,1", "a1", "a0", "m2", "a2", "b1", "m3,4", "a4", "a3", "b0", "b2", "c1", "b4", "m5,6", "a5", "a6",
-    "b3", "c0", "d1", "c2", "c4", "b5", "d0", "b6", "m7,8", "a8", "a7", "c3", "d2", "c5", "c6", "d4", "m9",
-    "a9", "b8", "d3", "b7", "m10", "a10", "b9", "d5", "c8", "d6", "c7", "m11", "c9", "b10", "d8", "b11",
-    "B11", "c10", "d7", "c11", "C11", "d9", "d10", "d11",
+    "m0,1", "a1", "a0", "m2", "a2", "b1", "b0", "m3,4", "a4", "a3", "b2", "c1", "c0", "b4", "b3", "m5,6",
+    "a5", "a6", "c2", "c4", "c3", "b5", "d1", "d0", "b6", "m7,8", "a8", "a7", "c5", "c6", "d2", "d4", "d3",
+    "m9", "a9", "b8", "b7", "d5", "m10", "a10", "c8", "c7", "b9", "d6", "m11", "c9", "b10", "d8", "d7", "b11",
+    "B11", "c10", "c11", "C11", "d9", "d10", "d11",
 )
 HALF = FEATS // 2
 

time: 88.2 us -> 87.6 us (level)
  no operation moved by 1% of the time
where the time goes in v3:
time: 87.6 us; the launch traced here: 87.5 us
  Pallas kernels  85.4 us (97%)
  local copies, waits for them, and re-layouts  2.14 us (2%)
    pallas_call x1, Pallas kernels, per_device(): pl.pallas_call(kernel, out_shape=jax.ShapeDtypeStruct((2, 64, SUBS * L),...  85.4 us

profile of v3, /device:TPU:5, one launch (start us, length us, event | category | flops | bytes accessed | tf_op | source)
XLA Modules:
  0.0 87.5 jit_solution(13727216534082244853)
XLA Ops:
  0.0 0.0 copy-start
  0.0 0.7 copy-done
  0.7 0.0 copy-start.1
  0.7 0.7 copy-done.1
  1.3 85.4 %shard_map.46 = f32[2,64,384]{2,1,0:T(8,128)S(1)} custom-call(bf16[2048,1024]{1,0:T(8,128)(2,1)} %tok_hbm.1, bf16[2048,384]{1,0:T(8,128)(2,1)} %cot_hbm.1, s32[1,2]{1,0:T(1,128)S(1)} %copy-done, s32[1,2]{1,0:T(1,128)S(1)} %copy-done.1), custom_call_target="tpu_custom_call" | custom-call | flops 6442450944 | bytes 6000000 | tf_op jit(solution)/shard_map/pallas_call | solution.py:284
  86.7 0.8 copy.5
Async XLA Ops:
  0.0 0.7 copy-start
  0.7 0.7 copy-start.1
